TPU v7x, 32 devices: a whole 2x2x4 slice. The times are simulated.
32 devices in a mesh: groups: 2 (over y), expert: 16 (over z, x, core).
Axes of the slice: x: 2, y: 2, z: 4, core: 2. Of those that a mesh axis runs over, the one named last changes fastest.
Arguments:
- attn_heads: bfloat16 [4096, 4096], P(('groups', 'expert')), parts along dimension 0, may hold values from -6 to 6
- residual: bfloat16 [4096, 2048], P(('groups', 'expert')), parts along dimension 0, may hold values from -6 to 6
- w_out: bfloat16 [4096, 2048], P('expert'), may hold values from -0.09375 to 0.09375
- norm_gain: float32 [2048], replicated, may hold values from 0.1 to 1.9
- expert_ids: int32 [4096, 8], P(('groups', 'expert')), parts along dimension 0, may hold values from 0 to 15, all different within a row; in each aligned block of 128 rows (0 to 127, 128 to 255, ...) at most 80 rows name the same one
- route_num: int32 [4096, 8], P(('groups', 'expert')), parts along dimension 0, may hold values from 1 to 16
- w_gate: bfloat16 [16, 2048, 768], P('expert'), may hold values from -0.125 to 0.125
- w_up: bfloat16 [16, 2048, 768], P('expert'), may hold values from -0.125 to 0.125
- w_down: bfloat16 [16, 768, 2048], P('expert'), may hold values from -0.21875 to 0.21875
Outputs:
- mid_state: bfloat16 [4096, 2048], P(('groups', 'expert')), parts along dimension 0
- expert_out: bfloat16 [4096, 2048], P(('groups', 'expert')), parts along dimension 0
There are 2 independent parts, one for each index of `groups`. A program takes and returns all parts, laid end to end along the dimension named above; an argument that names none is the same for every part. Nothing has to cross between parts.
Inputs may be any that keep to these rules, and one draw needn't show every extreme that they name: `expert_ids`: each token names 8 different experts; among the 128 tokens of one device no expert is named more than 80 times, a bound that some block reaches.
All inputs are finite; a program needn't handle non-finite values.
Results may differ from a plain program's by a relative error of at most 0.0095.
Values may be sent and summed in bfloat16 or wider, within the bound.
No kernel may reach another device: no remote copies, remote signals or barrier semaphores. Data moves between devices by JAX's collectives and lax.ppermute only.
A program may use at most 128 MiB of HBM per device.

v0:
```python
import jax
import jax.numpy as jnp
from jax import lax
from jax.sharding import PartitionSpec as P

epsilon = 1e-06


def rms_scale(tensor, norm_gain):
    values = tensor.astype(jnp.float32)
    mean_sq = jnp.mean(values * values, axis=-1, keepdims=True)
    return (values * lax.rsqrt(mean_sq + epsilon) * norm_gain).astype(jnp.bfloat16)


def per_device(attn_heads, residual, w_out, norm_gain, expert_ids, route_num, w_gate, w_up, w_down):
    tok_rows = attn_heads.shape[0]
    feature_count = residual.shape[1]
    gathered = lax.all_gather(w_out, "expert", axis=0, tiled=True)
    projected = jnp.dot(attn_heads, gathered, preferred_element_type=jnp.float32)
    mid_state = (residual.astype(jnp.float32) + projected).astype(jnp.bfloat16)
    n_experts = lax.axis_size("expert")
    top_count = expert_ids.shape[1]
    capacity = tok_rows * top_count * 5 // (4 * n_experts)
    flat_ids = expert_ids.reshape(-1)
    onehot = (flat_ids[:, None] == jnp.arange(n_experts, dtype=jnp.int32)[None, :]).astype(
        jnp.int32
    )
    before = jnp.cumsum(onehot, axis=0) - onehot
    slot_index = jnp.sum(before * onehot, axis=1)
    position = flat_ids * capacity + slot_index
    token_index = jnp.arange(tok_rows * top_count, dtype=jnp.int32) // top_count
    payload = rms_scale(mid_state, norm_gain)
    sendbuf = jnp.zeros((n_experts * capacity, feature_count), jnp.bfloat16)
    sendbuf = sendbuf.at[position].set(payload[token_index])
    sendbuf = sendbuf.reshape(n_experts, capacity, feature_count)
    received = lax.all_to_all(sendbuf, "expert", split_axis=0, concat_axis=0, tiled=True)
    sources, slot_count, _ = received.shape
    row_block = received.reshape(sources * slot_count, feature_count)
    gate_act = jnp.dot(row_block, w_gate[0], preferred_element_type=jnp.float32)
    up_act = jnp.dot(row_block, w_up[0], preferred_element_type=jnp.float32)
    hidden = (jax.nn.silu(gate_act) * up_act).astype(jnp.bfloat16)
    result = jnp.dot(hidden, w_down[0], preferred_element_type=jnp.float32).astype(jnp.bfloat16)
    result = result.reshape(sources, slot_count, feature_count)
    returned = lax.all_to_all(result, "expert", split_axis=0, concat_axis=0, tiled=True)
    returned = returned.reshape(n_experts * capacity, feature_count)
    picked = returned[position].astype(jnp.float32).reshape(tok_rows, top_count, feature_count)
    numer = route_num.astype(jnp.float32)
    weights = numer / jnp.sum(numer, axis=1, keepdims=True)
    expert_out = jnp.sum(picked * weights[:, :, None], axis=1).astype(jnp.bfloat16)
    return (mid_state, expert_out)


def solution(mesh):
    in_specs = (
        P(("groups", "expert"), None),
        P(("groups", "expert"), None),
        P("expert", None),
        P(),
        P(("groups", "expert"), None),
        P(("groups", "expert"), None),
        P("expert", None, None),
        P("expert", None, None),
        P("expert", None, None),
    )
    out_specs = (P(("groups", "expert"), None), P(("groups", "expert"), None))
    return jax.shard_map(
        per_device, mesh=mesh, in_specs=in_specs, out_specs=out_specs, check_vma=False
    )
```

profile of v0, /device:TPU:11, one launch (start us, length us, event | category | flops | bytes accessed | tf_op | source)
XLA Modules:
  0.0 452.5 jit_solution(2157559371774095986)
XLA Ops:
  7.2 0.0 copy-start
  7.2 0.0 all-gather.2.cloned.1.call-start
  7.2 0.7 all-gather.2.cloned.1.call-update
  7.9 1.0 copy.15
  8.9 0.1 eq.29
  9.0 0.1 eq.25
  9.1 0.7 broadcast_multiply_fusion
  9.8 0.1 copy.14
  9.9 0.1 mul.55
  10.0 4.5 reduce-window.6
  14.5 0.1 slice.12
  14.6 0.1 copy.17
  14.8 0.1 copy.18
  14.8 0.1 broadcast_add_fusion
  15.0 0.0 copy-start.3
  15.0 120.6 %all-gather.2.cloned.1.call-done = bf16[4096,2048]{1,0:T(8,128)(2,1)} async-done(((bf16[256,2048]{1,0:T(8,128)(2,1)}), bf16[4096,2048]{1,0:T(8,128)(2,1)}) %all-gather.2.cloned.1.call-update) | async-done | bytes 16777232 | tf_op jit(solution)/shard_map/all_gather | solution.py:18
  135.6 8.6 %fusion.10 = (f32[128]{0:T(128)S(1)}, bf16[128,2048]{1,0:T(8,128)(2,1)S(1)}) fusion(bf16[128,4096]{1,0:T(8,128)(2,1)} %param.9, bf16[4096,2048]{1,0:T(8,128)(2,1)} %all-gather.2.cloned.1.call-done, bf16[128,2048]{1,0:T(8,128)(2,1)} %param.10), kind=kOutput, calls=%fused_computation.19 | convolution fusion | flops 2149056512 | bytes 18874880 | tf_op jit(solution)/shard_map/dot_general | solution.py:19
  144.2 0.0 copy-start.1
  144.2 0.8 copy-done.1
  145.0 0.0 copy-done.3
  145.0 1.0 fusion.12
  146.0 23.5 %scatter_custom_fusion = bf16[1280,2048]{1,0:T(8,128)(2,1)} fusion(s32[1024]{0:T(1024)S(1)} %bitcast.50, bf16[128,2048]{1,0:T(8,128)(2,1)} %fusion.12, s32[1024]{0:T(1024)S(1)} %broadcast_clamp_fusion.1, bf16[]{:T(256)} %constant.29.clone.1), kind=kCustom, calls=%fused_computation.6 | custom fusion | bytes 5243392 | tf_op jit(solution)/shard_map/scatter | solution.py:34
  169.5 121.6 %all_to_all.10 = bf16[16,80,2048]{2,1,0:T(8,128)(2,1)S(1)} all-to-all(bf16[16,80,2048]{2,1,0:T(8,128)(2,1)} %bitcast.43), channel_id=1, replica_groups=mesh['groups'=2,'expert'=16] {'expert'}, dimensions={0} | all-to-all | bytes 10485760 | tf_op jit(solution)/shard_map/all_to_all | solution.py:36
  291.1 0.0 copy-done.4
  291.1 4.3 fusion.6
  295.4 4.8 %fusion.3 = bf16[1280,768]{1,0:T(8,128)(2,1)S(1)} fusion(bf16[1280,2048]{1,0:T(8,128)(2,1)S(1)} %bitcast.46, f32[1280,768]{1,0:T(8,128)S(1)} %fusion.6, bf16[1,2048,768]{2,1,0:T(8,128)(2,1)S(1)} %copy-done.5), kind=kOutput, calls=%fused_computation.9 | convolution fusion | flops 4032430080 | bytes 14286848 | tf_op jit(solution)/shard_map/dot_general | solution.py:40
  300.2 6.1 %convolution_convert_fusion = bf16[1280,2048]{1,0:T(8,128)(2,1)} fusion(bf16[1280,768]{1,0:T(8,128)(2,1)S(1)} %fusion.3, bf16[1,768,2048]{2,1,0:T(8,128)(2,1)S(1)} %copy-done), kind=kOutput, calls=%fused_computation.5 | convolution fusion | flops 4029153280 | bytes 10354688 | tf_op jit(solution)/shard_map/dot_general | solution.py:42
  306.3 5.1 %all-to-all-start.1 = ((bf16[16,80,2048]{2,1,0:T(8,128)(2,1)}), bf16[16,80,2048]{2,1,0:T(8,128)(2,1)}, u32[]{:S(2)}, u32[]{:S(2)}) async-start(bf16[16,80,2048]{2,1,0:T(8,128)(2,1)} %bitcast.44), calls=%async_computation.1 | async-start | bytes 10485760 | tf_op jit(solution)/shard_map/all_to_all | solution.py:44
  311.4 0.1 copy.19
  311.5 114.8 %all-to-all-done.1 = bf16[16,80,2048]{2,1,0:T(8,128)(2,1)} async-done(((bf16[16,80,2048]{2,1,0:T(8,128)(2,1)}), bf16[16,80,2048]{2,1,0:T(8,128)(2,1)}, u32[]{:S(2)}, u32[]{:S(2)}) %all-to-all-start.1) | async-done | bytes 5242912 | tf_op jit(solution)/shard_map/all_to_all | solution.py:44
  426.3 12.0 %gather_fusion = bf16[1024,2048]{1,0:T(8,128)(2,1)} fusion(bf16[1280,2048]{1,0:T(8,128)(2,1)} %bitcast.11, s32[1024]{0:T(1024)S(1)} %broadcast_clamp_fusion), kind=kCustom, calls=%fused_computation.1 | custom fusion | bytes 8392704 | tf_op jit(solution)/shard_map/gather | solution.py:46
  438.4 7.3 %fusion = bf16[128,2048]{1,0:T(8,128)(2,1)} fusion(bf16[1024,2048]{1,0:T(8,128)(2,1)} %gather_fusion, f32[128,8]{1,0:T(8,128)S(1)} %copy.19), kind=kLoop, calls=%fused_computation.4 | loop fusion | flops 6029312 | bytes 4722688 | tf_op jit(solution)/shard_map/reduce_sum | solution.py:49
  (17 shorter events, 0.1 us)
Async XLA Ops:
  7.2 293.1 %copy-start = (bf16[1,768,2048]{2,1,0:T(8,128)(2,1)S(1)}, bf16[1,768,2048]{2,1,0:T(8,128)(2,1)}, u32[]{:S(2)}) copy-start(bf16[1,768,2048]{2,1,0:T(8,128)(2,1)} %param.17) | copy-start | bytes 9437188
  7.2 128.4 %all-gather.2.cloned.1.call-start = ((), (), s32[]{:S(2)}) async-start(), calls=%async_computation.2 | async-start | bytes 17825792 | tf_op jit(solution)/shard_map/all_gather | solution.py:18
  15.0 130.0 %copy-start.3 = (f32[2048]{0:T(1024)S(1)}, f32[2048]{0:T(1024)}, u32[]{:S(2)}) copy-start(f32[2048]{0:T(1024)} %param.12) | copy-start | bytes 24580
  144.2 0.8 copy-start.1
  169.5 121.6 %copy-start.4 = (bf16[1,2048,768]{2,1,0:T(8,128)(2,1)S(1)}, bf16[1,2048,768]{2,1,0:T(8,128)(2,1)}, u32[]{:S(2)}) copy-start(bf16[1,2048,768]{2,1,0:T(8,128)(2,1)} %param.15) | copy-start | bytes 9437188
  291.1 4.3 copy-start.5
  306.3 5.1 %copy-start.2 = (s32[128,8]{0,1:T(8,128)S(1)}, s32[128,8]{0,1:T(8,128)}, u32[]{:S(2)}) copy-start(s32[128,8]{0,1:T(8,128)} %param.14) | copy-start | bytes 12292
  306.3 120.0 %all-to-all-start.1 = ((bf16[16,80,2048]{2,1,0:T(8,128)(2,1)}), bf16[16,80,2048]{2,1,0:T(8,128)(2,1)}, u32[]{:S(2)}, u32[]{:S(2)}) async-start(bf16[16,80,2048]{2,1,0:T(8,128)(2,1)} %bitcast.44), calls=%async_computation.1 | async-start | bytes 10485760 | tf_op jit(solution)/shard_map/all_to_all | solution.py:44
Sparse Core Ops, SparseCore 0:
  10.2 125.3 all-gather.1
where the time goes:
time: 453 us
  waiting for transfers between devices  236 us (52%)
  blocking collectives  122 us (27%)
  local copies, waits for them, and re-layouts  38.1 us (8%)
  matrix products  23.8 us (5%)
  between operations  14.2 us (3%)
  other arithmetic  13.7 us (3%)
  starting transfers between devices  5.1 us (1%)
    all_to_all x1, blocking collectives, per_device(): lax.all_to_all(sendbuf, 'expert', split_axis=0, concat_axis=0, tiled=True)  122 us
    all_gather x1, waiting for transfers between devices, per_device(): gathered = lax.all_gather(w_out, 'expert', axis=0, tiled=True)  121 us
    all_to_all x1, waiting for transfers between devices, per_device(): lax.all_to_all(result, 'expert', split_axis=0, concat_axis=0, tiled=True)  115 us
    scatter x1, local copies, waits for them, and re-layouts, per_device(): sendbuf = sendbuf.at[position].set(payload[token_index])  23.5 us
    gather x1, local copies, waits for them, and re-layouts, per_device(): returned[position].astype(jnp.float32)  12 us
  transfers between devices with their start and end apart: 2, of which 2 were waited for; matrix products, arithmetic and copies ran while one was open for 2% of the time, Pallas kernels for 0%

commit v1 on v0

--- a/solution.py
+++ b/solution.py
@@ -15,7 +15,9 @@
 def per_device(attn_heads, residual, w_out, norm_gain, expert_ids, route_num, w_gate, w_up, w_down):
     tok_rows = attn_heads.shape[0]
     feature_count = residual.shape[1]
-    gathered = lax.all_gather(w_out, "expert", axis=0, tiled=True)
+    gathered = jnp.concatenate(
+        lax.all_to_all(jnp.stack([w_out] * lax.axis_size("expert"), 0), "expert", 0, 0), 0
+    )
     projected = jnp.dot(attn_heads, gathered, preferred_element_type=jnp.float32)
     mid_state = (residual.astype(jnp.float32) + projected).astype(jnp.bfloat16)
     n_experts = lax.axis_size("expert")

time: 453 us -> 686 us (1.51)
  waiting for transfers between devices: 236 us -> 471 us
  between operations: 14.2 us -> 0.77 us
  starting transfers between devices: 5.1 us -> 12.1 us
    all_to_all x0 -> x1, waiting for transfers between devices: none -> 357 us  [per_device(): lax.all_to_all(jnp.stack([w_out] * lax.axis_size('expert'), 0), 'expert',...]
    all_gather x1 -> x0, waiting for transfers between devices: 121 us -> none  [per_device(): gathered = lax.all_gather(w_out, 'expert', axis=0, tiled=True)]
    another operation x2 -> x3, local copies, waits for them, and re-layouts: 0.08 us -> 7.09 us  [the longest x1 7.01 us: per_device(): jnp.stack([w_out] * lax.axis_size('expert'), 0)]
  transfers between devices with their start and end apart: 2 -> 2, of which waited for: 2 -> 2; matrix products, arithmetic and copies ran while one was open for 2% -> 1% of each run, Pallas kernels for 0% -> 0%
where the time goes in v1:
time: 686 us; the launch traced here: 685 us
  waiting for transfers between devices  471 us (69%)
  blocking collectives  120 us (17%)
  local copies, waits for them, and re-layouts  44.3 us (6%)
  matrix products  23.8 us (3%)
  other arithmetic  13 us (2%)
  starting transfers between devices  12.1 us (2%)
    all_to_all x1, waiting for transfers between devices, per_device(): lax.all_to_all(jnp.stack([w_out] * lax.axis_size('expert'), 0), 'expert',...  357 us
    all_to_all x1, blocking collectives, per_device(): lax.all_to_all(sendbuf, 'expert', split_axis=0, concat_axis=0, tiled=True)  120 us
    all_to_all x1, waiting for transfers between devices, per_device(): lax.all_to_all(result, 'expert', split_axis=0, concat_axis=0, tiled=True)  115 us
    scatter x1, local copies, waits for them, and re-layouts, per_device(): sendbuf = sendbuf.at[position].set(payload[token_index])  23.6 us
  transfers between devices with their start and end apart: 2, of which 2 were waited for; matrix products, arithmetic and copies ran while one was open for 1% of the time, Pallas kernels for 0%

profile of v1, /device:TPU:11, one launch (start us, length us, event | category | flops | bytes accessed | tf_op | source)
XLA Modules:
  0.0 685.1 jit_solution(15903869532167235633)
XLA Ops:
  0.6 0.0 copy-start
  0.6 7.0 %stack.2 = bf16[16,256,2048]{2,1,0:T(8,128)(2,1)} broadcast(bf16[256,2048]{1,0:T(8,128)(2,1)} %param.11), dimensions={1,2} | broadcast | bytes 17825792 | tf_op jit(solution)/shard_map/stack | solution.py:19
  7.7 6.7 all-to-all-start
  14.3 0.0 copy-done.2
  14.3 0.1 copy.15
  14.4 0.1 eq.29
  14.5 0.1 eq.25
  14.6 0.1 copy.14
  14.7 0.1 mul.55
  14.8 4.5 reduce-window.6
  19.3 0.1 slice.12
  19.4 0.1 copy.17
  19.6 0.1 copy.18
  19.7 0.1 broadcast_add_fusion
  19.8 356.6 %all-to-all-done = bf16[16,256,2048]{2,1,0:T(8,128)(2,1)} async-done(((bf16[16,256,2048]{2,1,0:T(8,128)(2,1)}), bf16[16,256,2048]{2,1,0:T(8,128)(2,1)}, u32[]{:S(2)}, u32[]{:S(2)}) %all-to-all-start) | async-done | bytes 16777248 | tf_op jit(solution)/shard_map/all_to_all | solution.py:19
  376.4 8.6 %fusion.10 = (f32[128]{0:T(128)S(1)}, bf16[128,2048]{1,0:T(8,128)(2,1)S(1)}) fusion(bf16[128,4096]{1,0:T(8,128)(2,1)} %param.9, bf16[4096,2048]{1,0:T(8,128)(2,1)} %bitcast, bf16[128,2048]{1,0:T(8,128)(2,1)} %param.10), kind=kOutput, calls=%fused_computation.19 | convolution fusion | flops 2149056512 | bytes 18874880 | tf_op jit(solution)/shard_map/dot_general | solution.py:21
  385.1 0.0 copy-start.1
  385.1 0.8 copy-done.1
  385.9 0.0 copy-done.4
  385.9 1.0 fusion.12
  386.8 23.6 %scatter_custom_fusion = bf16[1280,2048]{1,0:T(8,128)(2,1)} fusion(s32[1024]{0:T(1024)S(1)} %bitcast.50, bf16[128,2048]{1,0:T(8,128)(2,1)} %fusion.12, s32[1024]{0:T(1024)S(1)} %broadcast_clamp_fusion.1, bf16[]{:T(256)} %constant.29.clone.1), kind=kCustom, calls=%fused_computation.6 | custom fusion | bytes 5243392 | tf_op jit(solution)/shard_map/scatter | solution.py:36
  410.4 119.7 %all_to_all.15 = bf16[16,80,2048]{2,1,0:T(8,128)(2,1)S(1)} all-to-all(bf16[16,80,2048]{2,1,0:T(8,128)(2,1)} %bitcast.43), channel_id=1, replica_groups=mesh['groups'=2,'expert'=16] {'expert'}, dimensions={0} | all-to-all | bytes 10485760 | tf_op jit(solution)/shard_map/all_to_all | solution.py:38
  530.1 0.0 copy-done.5
  530.2 4.3 fusion.6
  534.5 4.8 fusion.3
  539.3 6.1 convolution_convert_fusion
  545.4 5.4 all-to-all-start.2
  550.8 0.0 copy-done.3
  550.8 0.1 copy.19
  551.0 114.8 %all-to-all-done.2 = bf16[16,80,2048]{2,1,0:T(8,128)(2,1)} async-done(((bf16[16,80,2048]{2,1,0:T(8,128)(2,1)}), bf16[16,80,2048]{2,1,0:T(8,128)(2,1)}, u32[]{:S(2)}, u32[]{:S(2)}) %all-to-all-start.2) | async-done | bytes 5242912 | tf_op jit(solution)/shard_map/all_to_all | solution.py:46
  665.7 12.0 %gather_fusion = bf16[1024,2048]{1,0:T(8,128)(2,1)} fusion(bf16[1280,2048]{1,0:T(8,128)(2,1)} %bitcast.12, s32[1024]{0:T(1024)S(1)} %broadcast_clamp_fusion), kind=kCustom, calls=%fused_computation.1 | custom fusion | bytes 8392704 | tf_op jit(solution)/shard_map/gather | solution.py:48
  677.8 7.3 %fusion = bf16[128,2048]{1,0:T(8,128)(2,1)} fusion(bf16[1024,2048]{1,0:T(8,128)(2,1)} %gather_fusion, f32[128,8]{1,0:T(8,128)S(1)} %copy.19), kind=kLoop, calls=%fused_computation.4 | loop fusion | flops 6029312 | bytes 4722688 | tf_op jit(solution)/shard_map/reduce_sum | solution.py:51
  (19 shorter events, 0.1 us)
Async XLA Ops:
  0.6 538.7 %copy-start = (bf16[1,768,2048]{2,1,0:T(8,128)(2,1)S(1)}, bf16[1,768,2048]{2,1,0:T(8,128)(2,1)}, u32[]{:S(2)}) copy-start(bf16[1,768,2048]{2,1,0:T(8,128)(2,1)} %param.17) | copy-start | bytes 9437188
  7.7 6.7 copy-start.2
  7.7 368.8 %all-to-all-start = ((bf16[16,256,2048]{2,1,0:T(8,128)(2,1)}), bf16[16,256,2048]{2,1,0:T(8,128)(2,1)}, u32[]{:S(2)}, u32[]{:S(2)}) async-start(bf16[16,256,2048]{2,1,0:T(8,128)(2,1)} %stack.2), calls=%async_computation | async-start | bytes 33554432 | tf_op jit(solution)/shard_map/all_to_all | solution.py:19
  376.4 9.4 %copy-start.4 = (f32[2048]{0:T(1024)S(1)}, f32[2048]{0:T(1024)}, u32[]{:S(2)}) copy-start(f32[2048]{0:T(1024)} %param.12) | copy-start | bytes 24580
  385.1 0.8 copy-start.1
  410.4 119.7 %copy-start.5 = (bf16[1,2048,768]{2,1,0:T(8,128)(2,1)S(1)}, bf16[1,2048,768]{2,1,0:T(8,128)(2,1)}, u32[]{:S(2)}) copy-start(bf16[1,2048,768]{2,1,0:T(8,128)(2,1)} %param.15) | copy-start | bytes 9437188
  530.2 4.3 copy-start.6
  545.4 5.4 copy-start.3
  545.4 120.4 %all-to-all-start.2 = ((bf16[16,80,2048]{2,1,0:T(8,128)(2,1)}), bf16[16,80,2048]{2,1,0:T(8,128)(2,1)}, u32[]{:S(2)}, u32[]{:S(2)}) async-start(bf16[16,80,2048]{2,1,0:T(8,128)(2,1)} %bitcast.44), calls=%async_computation.2 | async-start | bytes 10485760 | tf_op jit(solution)/shard_map/all_to_all | solution.py:46
